TPU v7x, 32 devices: a whole 2x2x4 slice. The times are simulated.
32 devices in a mesh: gx: 4 (over y, core), gy: 8 (over z, x).
Axes of the slice: x: 2, y: 2, z: 4, core: 2. Of those that a mesh axis runs over, the one named last changes fastest.
Arguments:
- emission: float32 [512, 8, 128], P(('gx', 'gy')), may hold values from 0.05 to 1
- reflectance: float32 [512, 8, 128], P(('gx', 'gy')), may hold values from 0.5 to 0.98
- form_factors: float32 [8192, 128, 128], P(('gx', 'gy')), as said below
- link_source: int32 [8192], P(('gx', 'gy')), may hold values from 0 to 511, as said below
- link_target: int32 [8192], P(('gx', 'gy')), may hold values from 0 to 511, as said below
- link_length: int32 [8192], P(('gx', 'gy')), may hold values from 32 to 128
- block_count: int32 [32], P(('gx', 'gy')), may hold values from 32 to 256, as said below
Outputs:
- solution: float32 [512, 8, 128], P(('gx', 'gy'))
- residual: float32 [512, 8, 128], P(('gx', 'gy'))
Inputs may be any that keep to these rules, and one draw needn't show every extreme that they name: `form_factors`: entries are nonnegative. `link_source`: block k's source is any cluster; among the blocks held by one device, all blocks whose sources lie on one same device name the same source cluster. `link_target`: block k's target is one of the clusters of the device holding it, clusters (k // 256) * 16 to (k // 256) * 16 + 15. `block_count`: some device has all 256 slots live.
All inputs are finite; a program needn't handle non-finite values.
Results may differ from a plain program's by a relative error of at most 0.0011.
Values sent between devices are 32-bit elements; how exact they have to be, the bound alone decides.
A program may use at most 64 MiB of HBM per device.

v0:
```python
import jax
import jax.numpy as jnp
from jax import lax
from jax.sharding import PartitionSpec as P
from jax.experimental import pallas as pl
from jax.experimental.pallas import tpu as pltpu

ITERS = 3
PHASES = 2 * ITERS + 1
CHUNK = 16
SLOTS = 4
UNROLL = 128
EARLY = 4


def divide(x, by):
    if by & (by - 1) == 0:
        return lax.shift_right_logical(x, by.bit_length() - 1), lax.bitwise_and(x, by - 1)
    return lax.div(x, by), lax.rem(x, by)


def kernel(len_s, count_s, source_v, target_v, count_v, em, refl, ff, sol, res,
           w, stage, runs, vt, outb, inb, dout, din, image, direction, total, rs, ds, ims,
           wout, win, want_s, ints_v, ints_s, reals_v, reals_s,
           stage_sem, send_sem, recv_sem, wsend_sem, wrecv_sem, small_sem):
    nx, ny = lax.axis_size("gx"), lax.axis_size("gy")
    n = nx * ny
    me = lax.axis_index("gx") * ny + lax.axis_index("gy")
    clusters = em.shape[0]
    blocks, cl = ff.shape[0], ff.shape[2]
    chunks = blocks // CHUNK
    f32, bf16 = jnp.float32, jnp.bfloat16

    def fetch(c, slot):
        return pltpu.make_async_copy(ff.at[pl.ds(c * CHUNK, CHUNK)], stage.at[slot], stage_sem.at[slot])

    for c in range(min(SLOTS, chunks)):
        fetch(c, c).start()

    barrier = pltpu.get_barrier_semaphore()

    i32 = jnp.int32
    lane = lax.broadcasted_iota(i32, (1, 128), 1)
    gx, gy = lax.axis_index("gx"), lax.axis_index("gy")

    def each_peer(act):
        def some(t, carry):
            for a in range(nx):
                act(lax.rem(gx + a, nx), lax.rem(gy + ny - 1 - t, ny))
            return carry

        lax.fori_loop(0, ny - 1, some, 0)
        for a in range(1, nx):
            act(lax.rem(gx + a, nx), gy)

    each_peer(lambda px, py: pl.semaphore_signal(
        barrier, inc=1, device_id=(px, py), device_id_type=pl.DeviceIdType.MESH))

    owner, slot = divide(source_v[...], clusters)
    target = target_v[...] - me * clusters
    ids = lax.broadcasted_iota(i32, (1, blocks), 1)
    peers = lax.broadcasted_iota(i32, (n, blocks), 0)
    alive = jnp.broadcast_to(ids < count_v[:, 0:1], (n, blocks))
    match = jnp.logical_and(owner == peers, alive)
    wanted = jnp.max(jnp.where(match, jnp.broadcast_to(slot, (n, blocks)), 0), axis=1, keepdims=True)
    wout[...] = jnp.broadcast_to(wanted, (n, 128)).reshape(n, 1, 128)
    pl.semaphore_wait(barrier, n - 1)

    each_peer(lambda px, py: pltpu.make_async_remote_copy(
        src_ref=wout.at[px * ny + py], dst_ref=win.at[me], send_sem=wsend_sem, recv_sem=wrecv_sem,
        device_id=(px, py), device_id_type=pl.DeviceIdType.MESH).start())
    win[me] = wout[me]

    square_of = (blocks, blocks)
    down = lax.broadcasted_iota(i32, square_of, 0)
    across = lax.broadcasted_iota(i32, square_of, 1)

    def upright(row):
        return jnp.sum(jnp.where(down == across, jnp.broadcast_to(row, square_of), 0), axis=1, keepdims=True)

    key = target * blocks + ids
    key_up, owner_up, target_up = upright(key), upright(owner), upright(target)
    rank = jnp.sum((jnp.broadcast_to(key, square_of) < key_up).astype(i32), axis=1, keepdims=True)
    placed = rank == across

    def ordered(column):
        return jnp.sum(jnp.where(placed, column, 0), axis=0, keepdims=True)

    sorted_target = ordered(jnp.broadcast_to(target_up, square_of))
    ints_v[...] = jnp.zeros(ints_v.shape, i32)
    reals_v[...] = jnp.zeros(reals_v.shape, f32)
    ints_v[0:1, :] = ordered(down)
    ints_v[1:2, :] = ordered(jnp.broadcast_to(owner_up, square_of))
    up_to = jnp.sum((target_up <= across).astype(i32), axis=0, keepdims=True)
    same = jnp.sum((target_up == across).astype(i32), axis=0, keepdims=True)
    ints_v[2:3, :] = jnp.maximum(up_to - 1, 0)
    shifted = pltpu.roll(jnp.broadcast_to(sorted_target, (8, blocks)), 1, 1)[0:1]
    joined = jnp.logical_and(shifted == sorted_target, ids > 0)
    reals_v[0:1, :] = jnp.where(joined, 1.0, 0.0)
    reals_v[1:2, :] = jnp.where(same > 0, 1.0, 0.0)
    small = (pltpu.make_async_copy(ints_v, ints_s, small_sem.at[0]),
             pltpu.make_async_copy(reals_v, reals_s, small_sem.at[1]))
    for copy in small:
        copy.start()

    def fold(pairs):
        row = jnp.zeros((1, 128), f32)
        for i, (a, b) in enumerate(pairs):
            part = jnp.sum(a[...] * b[...], axis=0)
            part = part + pltpu.roll(part, 64, 1)
            part = part + pltpu.roll(part, 32, 1)
            part = jnp.sum(part, axis=0, keepdims=True)
            row = jnp.where(lane // 32 == i, part, row)
        return row

    def send(phase, field, pairs):
        row = fold(pairs)
        if field is None:
            dout[...] = row
            din[me] = row
        else:
            inb[phase, me, 0:8] = field[want_s[me, 0, 0]]
            inb[phase, me, 8:9] = row

        def one(px, py):
            peer = px * ny + py
            if field is None:
                src, dst = dout, din.at[me]
            else:
                outb[phase, peer, 0:8] = field[want_s[peer, 0, 0]]
                outb[phase, peer, 8:9] = row
                src, dst = outb.at[phase, peer], inb.at[phase, me]
            pltpu.make_async_remote_copy(
                src_ref=src, dst_ref=dst, send_sem=send_sem.at[phase], recv_sem=recv_sem.at[phase],
                device_id=(px, py), device_id_type=pl.DeviceIdType.MESH).start()

        each_peer(one)

    def drain(ref, sem):
        part = ref.at[pl.ds(0, n - 1)]
        pltpu.make_async_copy(part, part, sem).wait()

    def receive(phase, rows):
        if rows:
            drain(inb.at[phase], recv_sem.at[phase])
            drain(outb.at[phase], send_sem.at[phase])
            return inb[phase, :, 8, :]
        drain(din, recv_sem.at[phase])
        drain(din, send_sem.at[phase])
        return din[...].reshape(n, 128)

    def whole(parts, i):
        column = jnp.sum(parts, axis=0, keepdims=True)
        return jnp.broadcast_to(
            jnp.sum(jnp.where(lane // 32 == i, column, 0.0), axis=1, keepdims=True), (8, 128))

    def put_sources(v):
        low = v - v.astype(bf16).astype(f32)
        vt[...] = jnp.concatenate([v, low], axis=1).astype(bf16)

    def apply(v):
        def step(s, acc):
            for u in range(UNROLL // 2):
                r = s * UNROLL + 2 * u
                va, vb = vt[ints_s[1, r]], vt[ints_s[1, r + 1]]
                left = jnp.concatenate([jnp.concatenate([va, va], axis=1),
                                        jnp.concatenate([vb, vb], axis=1)], axis=0)
                right = jnp.concatenate([w[ints_s[0, r]], w[ints_s[0, r + 1]]], axis=1)
                out = jnp.dot(left, right, preferred_element_type=f32)
                acc = acc * reals_s[0, r] + (out[0:8, :cl] + out[8:16, :cl])
                runs[r] = acc
                acc = acc * reals_s[0, r + 1] + (out[16:24, cl:] + out[24:32, cl:])
                runs[r + 1] = acc
            return acc

        lax.fori_loop(0, blocks // UNROLL, step, jnp.zeros((8, cl), f32))
        g = jnp.stack([runs[ints_s[2, t]] * reals_s[1, t] for t in range(clusters)])
        return v - refl[...] * g

    def prepare(c, carry):
        slot = lax.rem(c, SLOTS)
        fetch(c, slot).wait()

        def block(b, inner):
            k = c * CHUNK + b
            t = stage[slot, b].T
            j = lax.broadcasted_iota(jnp.int32, (cl, cl), 0)
            t = jnp.where(j < jnp.where(k < count_s[0], len_s[k], 0), t, 0.0)
            high = t.astype(bf16)
            w[k, 0:cl] = high
            w[k, cl:2 * cl] = (t - high.astype(f32)).astype(bf16)
            return inner

        lax.fori_loop(0, CHUNK, block, 0, unroll=4)

        @pl.when(c + SLOTS < chunks)
        def _():
            fetch(c + SLOTS, slot).start()

        return carry

    early = min(EARLY, chunks)
    lax.fori_loop(0, early, prepare, 0)
    drain(win, wrecv_sem)
    drain(wout, wsend_sem)
    asked = pltpu.make_async_copy(win, want_s, small_sem.at[2])
    asked.start()
    asked.wait()
    send(0, em, [(em, em)])
    lax.fori_loop(early, chunks, prepare, 0)
    for copy in small:
        copy.wait()

    rho = whole(receive(0, True), 0)
    rs[...] = inb[0, :, 0:8, :]
    res[...] = em[...]
    rho_old, alpha, omega = None, None, None
    for it in range(ITERS):
        last = it == ITERS - 1
        if it == 0:
            direction[...] = em[...]
            ds[...] = rs[...]
        else:
            beta = rho / rho_old * (alpha / omega)
            direction[...] = res[...] + beta * (direction[...] - omega * image[...])
            ds[...] = rs[...] + beta * (ds[...] - omega * ims[...])
        put_sources(ds[...])
        image[...] = apply(direction[...])
        phase = 1 + 2 * it
        send(phase, image, [(em, image)])
        alpha = rho / whole(receive(phase, True), 0)
        ims[...] = inb[phase, :, 0:8, :]
        res[...] = res[...] - alpha * image[...]
        rs[...] = rs[...] - alpha * ims[...]
        put_sources(rs[...])
        sol[...] = apply(res[...])
        send(phase + 1, None if last else sol, [(sol, res), (sol, sol), (em, res), (em, sol)])
        parts = receive(phase + 1, not last)
        omega = whole(parts, 0) / whole(parts, 1)
        if it == 0:
            total[...] = alpha * direction[...] + omega * res[...]
        else:
            total[...] = total[...] + alpha * direction[...] + omega * res[...]
        res[...] = res[...] - omega * sol[...]
        if not last:
            rs[...] = rs[...] - omega * inb[phase + 1, :, 0:8, :]
        rho_old = rho
        rho = whole(parts - omega[0:1] * pltpu.roll(parts, 96, 1), 2)
    sol[...] = total[...]


def local(emission, reflectance, form_factors, link_source, link_target, link_length, block_count):
    clusters, bands, cl = emission.shape
    blocks = form_factors.shape[0]
    devices = lax.axis_size(("gx", "gy"))
    i32, f32, bf16 = jnp.int32, jnp.float32, jnp.bfloat16
    smem = pl.BlockSpec(memory_space=pltpu.SMEM)
    vmem = pl.BlockSpec(memory_space=pltpu.VMEM)
    field = (clusters, bands, cl)
    rows = (devices, bands, cl)
    dma = pltpu.SemaphoreType.DMA
    return pl.pallas_call(
        kernel,
        out_shape=[jax.ShapeDtypeStruct(field, f32)] * 2,
        in_specs=[smem] * 2 + [vmem] * 5 + [pl.BlockSpec(memory_space=pl.ANY)],
        out_specs=[vmem, vmem],
        scratch_shapes=[
            pltpu.VMEM((blocks, 2 * cl, cl), bf16),
            pltpu.VMEM((SLOTS, CHUNK, cl, cl), f32),
            pltpu.VMEM((blocks, bands, cl), f32),
            pltpu.VMEM((devices, 2 * bands, cl), bf16),
            pltpu.VMEM((PHASES - 1, devices, bands + 1, cl), f32),
            pltpu.VMEM((PHASES - 1, devices, bands + 1, cl), f32),
            pltpu.VMEM((1, 128), f32),
            pltpu.VMEM((devices, 1, 128), f32),
            pltpu.VMEM(field, f32),
            pltpu.VMEM(field, f32),
            pltpu.VMEM(field, f32),
            pltpu.VMEM(rows, f32),
            pltpu.VMEM(rows, f32),
            pltpu.VMEM(rows, f32),
            pltpu.VMEM((devices, 1, 128), i32),
            pltpu.VMEM((devices, 1, 128), i32),
            pltpu.SMEM((devices, 1, 128), i32),
            pltpu.VMEM((8, blocks), i32),
            pltpu.SMEM((8, blocks), i32),
            pltpu.VMEM((8, blocks), f32),
            pltpu.SMEM((8, blocks), f32),
            dma((SLOTS,)),
            dma((PHASES,)),
            dma((PHASES,)),
            dma,
            dma,
            dma((3,)),
        ],
        compiler_params=pltpu.CompilerParams(
            collective_id=0, has_side_effects=True, vmem_limit_bytes=56 * 1024 * 1024),
        name="radiosity",
    )(link_length, block_count, link_source.reshape(1, blocks), link_target.reshape(1, blocks),
      block_count.reshape(1, 1), emission, reflectance, form_factors)


def solution(mesh):
    wide = P(("gx", "gy"), None, None)
    flat = P(("gx", "gy"))
    return jax.shard_map(local, mesh=mesh, in_specs=(wide, wide, wide, flat, flat, flat, flat),
                         out_specs=(wide, wide), check_vma=False)
```

profile of v0, /device:TPU:0, one launch (start us, length us, event | category | flops | bytes accessed | tf_op | source)
XLA Modules:
  0.0 77.6 jit_solution(14429349432093076950)
XLA Ops:
  1.3 73.3 %radiosity.1 = (f32[16,8,128]{2,1,0:T(8,128)}, f32[16,8,128]{2,1,0:T(8,128)}) custom-call(s32[256]{0:T(256)} %len_s.1, s32[1]{0:T(128)} %copy.11.count_s, s32[1,256]{1,0:T(1,128)} %bitcast.4, s32[1,256]{1,0:T(1,128)} %bitcast.5, s32[1,1]{1,0:T(1,128)} %bitcast.3.count_v, f32[16,8,128]{2,1,0:T(8,128)} %em.1, f32[16,8,128]{2,1,0:T(8,128)} %refl.1, ...), custom_call_target="tpu_custom_call" | custom-call | tf_op jit(solution)/shard_map/radiosity/pallas_call | solution.py:262
  74.6 1.5 %copy.12 = f32[16,8,128]{2,1,0:T(8,128)} copy(f32[16,8,128]{2,1,0:T(8,128)} %get-tuple-element.4) | data formatting | bytes 131072
  76.1 1.5 %copy.13 = f32[16,8,128]{2,1,0:T(8,128)} copy(f32[16,8,128]{2,1,0:T(8,128)} %get-tuple-element.5) | data formatting | bytes 131072
where the time goes:
time: 77.9 us; the launch traced here: 77.6 us
  Pallas kernels  73.3 us (94%)
  local copies, waits for them, and re-layouts  2.95 us (4%)
  between operations  1.29 us (2%)
    pallas_call x1, Pallas kernels, local(): pl.pallas_call(kernel, out_shape=[jax.ShapeDtypeStruct(field, f32)] * 2,...  73.3 us
    unnamed x2, local copies, waits for them, and re-layouts  2.95 us

commit v1 on v0

v1 whole, which is shorter than its diff:
```python
import jax
import jax.numpy as jnp
from jax import lax
from jax.sharding import PartitionSpec as P
from jax.experimental import pallas as pl
from jax.experimental.pallas import tpu as pltpu

ITERS = 3
PHASES = 2 * ITERS + 1
CHUNK = 16
SLOTS = 4
UNROLL = 128
EARLY = 6


def divide(x, by):
    if by & (by - 1) == 0:
        return lax.shift_right_logical(x, by.bit_length() - 1), lax.bitwise_and(x, by - 1)
    return lax.div(x, by), lax.rem(x, by)


def partners(index, size):
    if size & (size - 1):
        return [lax.rem(index + a, size) for a in range(size)]
    flips = [(1 << b) - 2 * (1 << b) * lax.rem(lax.div(index, 1 << b), 2) for b in range(size.bit_length() - 1)]
    out = []
    for a in range(size):
        p = index
        for b, flip in enumerate(flips):
            if a >> b & 1:
                p = p + flip
        out.append(p)
    return out


def kernel(len_h, count_h, source_h, target_h, em_h, refl_h, ff, sol, res,
           w, stage, runs, vt, outb, inb, dout, din, em, refl, image, direction, total, rs, ds,
           wout, win, want_s, ints_v, ints_s, reals_v, reals_s, source_v, target_v, len_s, count_s,
           stage_sem, send_sem, recv_sem, ssend_sem, srecv_sem, wsend_sem, wrecv_sem, small_sem):
    nx, ny = lax.axis_size("gx"), lax.axis_size("gy")
    n = nx * ny
    gx, gy = lax.axis_index("gx"), lax.axis_index("gy")
    me = gx * ny + gy
    clusters = em.shape[0]
    blocks, cl = ff.shape[0], ff.shape[2]
    chunks = blocks // CHUNK
    i32, f32, bf16 = jnp.int32, jnp.float32, jnp.bfloat16

    pxs, pys = partners(gx, nx), partners(gy, ny)
    order = sorted(
        ((a, b) for a in range(nx) for b in range(ny) if a or b),
        key=lambda q: (-bin(q[0] >> 1).count("1") - (q[1] & 1), -(q[0] & 1), -q[1]))

    def each_peer(act):
        for a, b in order:
            act(pxs[a], pys[b])

    barrier = pltpu.get_barrier_semaphore()
    each_peer(lambda px, py: pl.semaphore_signal(
        barrier, inc=1, device_id=(px, py), device_id_type=pl.DeviceIdType.MESH))

    def fetch(c, slot):
        return pltpu.make_async_copy(ff.at[pl.ds(c * CHUNK, CHUNK)], stage.at[slot], stage_sem.at[slot])

    inputs = [pltpu.make_async_copy(src, dst, small_sem.at[3 + i]) for i, (src, dst) in enumerate((
        (source_h, source_v), (target_h, target_v), (count_h, count_s), (len_h, len_s), (em_h, em), (refl_h, refl)))]
    for copy in inputs[:4]:
        copy.start()
    for c in range(min(SLOTS, chunks)):
        fetch(c, c).start()
    for copy in inputs[4:]:
        copy.start()

    lane = lax.broadcasted_iota(i32, (1, 128), 1)

    for copy in inputs[:4]:
        copy.wait()
    owner, slot = divide(source_v[...], clusters)
    target = target_v[...] - me * clusters
    ids = lax.broadcasted_iota(i32, (1, blocks), 1)
    peers = lax.broadcasted_iota(i32, (n, blocks), 0)
    alive = jnp.broadcast_to(ids < count_s[0], (n, blocks))
    match = jnp.logical_and(owner == peers, alive)
    wanted = jnp.max(jnp.where(match, jnp.broadcast_to(slot, (n, blocks)), 0), axis=1, keepdims=True)
    wout[...] = jnp.broadcast_to(wanted, (n, 128)).reshape(n, 1, 128)
    pl.semaphore_wait(barrier, n - 1)

    each_peer(lambda px, py: pltpu.make_async_remote_copy(
        src_ref=wout.at[px * ny + py], dst_ref=win.at[me], send_sem=wsend_sem, recv_sem=wrecv_sem,
        device_id=(px, py), device_id_type=pl.DeviceIdType.MESH).start())
    win[me] = wout[me]

    square_of = (blocks, blocks)
    down = lax.broadcasted_iota(i32, square_of, 0)
    across = lax.broadcasted_iota(i32, square_of, 1)

    def upright(row):
        return jnp.sum(jnp.where(down == across, jnp.broadcast_to(row, square_of), 0), axis=1, keepdims=True)

    key = target * blocks + ids
    key_up, owner_up, target_up = upright(key), upright(owner), upright(target)
    rank = jnp.sum((jnp.broadcast_to(key, square_of) < key_up).astype(i32), axis=1, keepdims=True)
    placed = rank == across

    def ordered(column):
        return jnp.sum(jnp.where(placed, column, 0), axis=0, keepdims=True)

    sorted_target = ordered(jnp.broadcast_to(target_up, square_of))
    ints_v[...] = jnp.zeros(ints_v.shape, i32)
    reals_v[...] = jnp.zeros(reals_v.shape, f32)
    ints_v[0:1, :] = ordered(down)
    ints_v[1:2, :] = ordered(jnp.broadcast_to(owner_up, square_of))
    up_to = jnp.sum((target_up <= across).astype(i32), axis=0, keepdims=True)
    same = jnp.sum((target_up == across).astype(i32), axis=0, keepdims=True)
    ints_v[2:3, :] = jnp.maximum(up_to - 1, 0)
    shifted = pltpu.roll(jnp.broadcast_to(sorted_target, (8, blocks)), 1, 1)[0:1]
    joined = jnp.logical_and(shifted == sorted_target, ids > 0)
    reals_v[0:1, :] = jnp.where(joined, 1.0, 0.0)
    reals_v[1:2, :] = jnp.where(same > 0, 1.0, 0.0)
    small = (pltpu.make_async_copy(ints_v, ints_s, small_sem.at[0]),
             pltpu.make_async_copy(reals_v, reals_s, small_sem.at[1]))
    for copy in small:
        copy.start()

    def fold(pairs):
        parts = [jnp.sum(a * b, axis=0) for a, b in pairs]
        if len(parts) == 1:
            return jnp.sum(parts[0], axis=0, keepdims=True)
        row = jnp.zeros((1, 128), f32)
        for i, part in enumerate(parts):
            part = part + pltpu.roll(part, 64, 1)
            part = part + pltpu.roll(part, 32, 1)
            row = jnp.where(lane // 32 == i, jnp.sum(part, axis=0, keepdims=True), row)
        return row

    def send(phase, pick):
        def one(px, py):
            peer = px * ny + py
            outb[phase, peer] = pick(peer)
            pltpu.make_async_remote_copy(
                src_ref=outb.at[phase, peer], dst_ref=inb.at[phase, me],
                send_sem=send_sem.at[phase], recv_sem=recv_sem.at[phase],
                device_id=(px, py), device_id_type=pl.DeviceIdType.MESH).start()

        each_peer(one)
        inb[phase, me] = pick(me)

    def send_sums(phase, pairs):
        row = fold(pairs)
        dout[phase] = row
        each_peer(lambda px, py: pltpu.make_async_remote_copy(
            src_ref=dout.at[phase], dst_ref=din.at[phase, me],
            send_sem=ssend_sem.at[phase], recv_sem=srecv_sem.at[phase],
            device_id=(px, py), device_id_type=pl.DeviceIdType.MESH).start())
        din[phase, me] = row

    def drain(ref, sem):
        part = ref.at[pl.ds(0, n - 1)]
        pltpu.make_async_copy(part, part, sem).wait()

    def receive(phase):
        drain(inb.at[phase], recv_sem.at[phase])
        drain(outb.at[phase], send_sem.at[phase])

    def sums(phase, count):
        drain(din.at[phase], srecv_sem.at[phase])
        drain(din.at[phase], ssend_sem.at[phase])
        column = jnp.sum(din[phase], axis=0)
        out = []
        for i in range(count):
            part = column if count == 1 else jnp.where(lane // 32 == i, column, 0.0)
            out.append(jnp.broadcast_to(jnp.sum(part, axis=1, keepdims=True), (8, 128)))
        return out

    def put_sources(v):
        low = v - v.astype(bf16).astype(f32)
        vt[...] = jnp.concatenate([v, low], axis=1).astype(bf16)

    def apply(v):
        blank = jnp.zeros((16, cl), bf16)

        def step(s, acc):
            for u in range(UNROLL // 4):
                r = s * UNROLL + 4 * u
                va, vb, vc, vd = (vt[ints_s[1, r + j]] for j in range(4))
                wa, wb, wc, wd = (w[ints_s[0, r + j]] for j in range(4))
                left = jnp.concatenate([
                    jnp.concatenate([va, blank], axis=1), jnp.concatenate([blank, vb], axis=1),
                    jnp.concatenate([vc, blank], axis=1), jnp.concatenate([blank, vd], axis=1)], axis=0)
                right = jnp.concatenate([
                    jnp.concatenate([wa, wb], axis=0), jnp.concatenate([wc, wd], axis=0)], axis=1)
                out = jnp.dot(left, right, preferred_element_type=f32)
                for j in range(4):
                    half = out[:, 0:cl] if j < 2 else out[:, cl:2 * cl]
                    acc = acc * reals_s[0, r + j] + (half[16 * j:16 * j + 8] + half[16 * j + 8:16 * j + 16])
                    runs[r + j] = acc
            return acc

        lax.fori_loop(0, blocks // UNROLL, step, jnp.zeros((8, cl), f32))
        g = jnp.stack([runs[ints_s[2, t]] * reals_s[1, t] for t in range(clusters)])
        return v - refl[...] * g

    def prepare(c, carry):
        slot = lax.rem(c, SLOTS)
        fetch(c, slot).wait()

        def block(b, inner):
            k = c * CHUNK + b
            t = stage[slot, b].T
            limit = jnp.where(k < count_s[0], len_s[k], 0)
            j = lax.broadcasted_iota(jnp.int32, (16, cl), 0)
            error = jnp.zeros((16, cl), f32)
            for m in range(0, cl, 16):
                x = jnp.where(j < limit - m, t[m:m + 16] + error, 0.0)
                q = x.astype(bf16)
                w[k, m:m + 16] = q
                error = x - q.astype(f32)
            return inner

        lax.fori_loop(0, CHUNK, block, 0, unroll=4)

        @pl.when(c + SLOTS < chunks)
        def _():
            fetch(c + SLOTS, slot).start()

        return carry

    for copy in inputs[4:]:
        copy.wait()
    early = min(EARLY, chunks)
    lax.fori_loop(0, early, prepare, 0)
    drain(win, wrecv_sem)
    drain(wout, wsend_sem)
    asked = pltpu.make_async_copy(win, want_s, small_sem.at[2])
    asked.start()

    def chosen(peer):
        slots = jnp.broadcast_to(win[peer], (8, 128))
        v = em[0]
        for c in range(1, clusters):
            v = jnp.where(slots == c, em[c], v)
        return v

    send(0, chosen)
    send_sums(0, [(em[...], em[...])])
    lax.fori_loop(early, chunks, prepare, 0)
    for copy in small:
        copy.wait()
    asked.wait()

    receive(0)
    rs[...] = inb[0]
    res[...] = em[...]
    rho, rho_old, alpha, omega = None, None, None, None
    for it in range(ITERS):
        last = it == ITERS - 1
        if it == 0:
            direction[...] = em[...]
            ds[...] = rs[...]
        else:
            beta = rho / rho_old * (alpha / omega)
            direction[...] = res[...] + beta * (direction[...] - omega * image[...])
            ds[...] = rs[...] + beta * (ds[...] - omega * inb[2 * it - 1])
        put_sources(ds[...])
        image[...] = apply(direction[...])
        phase = 1 + 2 * it
        send(phase, lambda peer: image[want_s[peer, 0, 0]])
        send_sums(phase, [(em[...], image[...])])
        if it == 0:
            rho, = sums(0, 1)
        receive(phase)
        alpha = rho / sums(phase, 1)[0]
        rs[...] = rs[...] - alpha * inb[phase]
        put_sources(rs[...])
        res[...] = res[...] - alpha * image[...]
        sol[...] = apply(res[...])
        phase = phase + 1
        if not last:
            send(phase, lambda peer: sol[want_s[peer, 0, 0]])
        send_sums(phase, [(sol[...], res[...]), (sol[...], sol[...]), (em[...], res[...]), (em[...], sol[...])])
        if it == 0:
            total[...] = alpha * direction[...]
        else:
            total[...] = total[...] + alpha * direction[...]
        if not last:
            receive(phase)
        tm, tt, sm, st = sums(phase, 4)
        omega = tm / tt
        rho_old, rho = rho, sm - omega * st
        total[...] = total[...] + omega * res[...]
        res[...] = res[...] - omega * sol[...]
        if not last:
            rs[...] = rs[...] - omega * inb[phase]
    sol[...] = total[...]


def local(emission, reflectance, form_factors, link_source, link_target, link_length, block_count):
    clusters, bands, cl = emission.shape
    blocks = form_factors.shape[0]
    devices = lax.axis_size(("gx", "gy"))
    i32, f32, bf16 = jnp.int32, jnp.float32, jnp.bfloat16
    vmem = pl.BlockSpec(memory_space=pltpu.VMEM)
    field = (clusters, bands, cl)
    rows = (devices, bands, cl)
    dma = pltpu.SemaphoreType.DMA
    return pl.pallas_call(
        kernel,
        out_shape=[jax.ShapeDtypeStruct(field, f32)] * 2,
        in_specs=[pl.BlockSpec(memory_space=pl.ANY)] * 7,
        out_specs=[vmem, vmem],
        scratch_shapes=[
            pltpu.VMEM((blocks, cl, cl), bf16),
            pltpu.VMEM((SLOTS, CHUNK, cl, cl), f32),
            pltpu.VMEM((blocks, bands, cl), f32),
            pltpu.VMEM((devices, 2 * bands, cl), bf16),
            pltpu.VMEM((PHASES - 1, devices, bands, cl), f32),
            pltpu.VMEM((PHASES - 1, devices, bands, cl), f32),
            pltpu.VMEM((PHASES, 1, 128), f32),
            pltpu.VMEM((PHASES, devices, 1, 128), f32),
            pltpu.VMEM(field, f32),
            pltpu.VMEM(field, f32),
            pltpu.VMEM(field, f32),
            pltpu.VMEM(field, f32),
            pltpu.VMEM(field, f32),
            pltpu.VMEM(rows, f32),
            pltpu.VMEM(rows, f32),
            pltpu.VMEM((devices, 1, 128), i32),
            pltpu.VMEM((devices, 1, 128), i32),
            pltpu.SMEM((devices, 1, 128), i32),
            pltpu.VMEM((8, blocks), i32),
            pltpu.SMEM((8, blocks), i32),
            pltpu.VMEM((8, blocks), f32),
            pltpu.SMEM((8, blocks), f32),
            pltpu.VMEM((1, blocks), i32),
            pltpu.VMEM((1, blocks), i32),
            pltpu.SMEM((blocks,), i32),
            pltpu.SMEM((1,), i32),
            dma((SLOTS,)),
            dma((PHASES - 1,)),
            dma((PHASES - 1,)),
            dma((PHASES,)),
            dma((PHASES,)),
            dma,
            dma,
            dma((9,)),
        ],
        compiler_params=pltpu.CompilerParams(
            collective_id=0, has_side_effects=True, vmem_limit_bytes=VMEM_LIMIT),
        name="radiosity",
    )(link_length, block_count, link_source.reshape(1, blocks), link_target.reshape(1, blocks),
      emission, reflectance, form_factors)


VMEM_LIMIT = 56 * 1024 * 1024


def solution(mesh):
    wide = P(("gx", "gy"), None, None)
    flat = P(("gx", "gy"))
    return jax.shard_map(local, mesh=mesh, in_specs=(wide, wide, wide, flat, flat, flat, flat),
                         out_specs=(wide, wide), check_vma=False)
```

time: 77.9 us -> 67.3 us (0.86)
  Pallas kernels: 73.3 us -> 62.9 us
    pallas_call x1, Pallas kernels: 73.3 us -> 62.9 us  [local(): pl.pallas_call(kernel, out_shape=[jax.ShapeDtypeStruct(field, f32)] * 2,...]
where the time goes in v1:
time: 67.3 us; the launch traced here: 67.1 us
  Pallas kernels  62.9 us (93%)
  local copies, waits for them, and re-layouts  2.95 us (4%)
  between operations  1.29 us (2%)
    pallas_call x1, Pallas kernels, local(): pl.pallas_call(kernel, out_shape=[jax.ShapeDtypeStruct(field, f32)] * 2,...  62.9 us
    unnamed x2, local copies, waits for them, and re-layouts  2.95 us

profile of v1, /device:TPU:0, one launch (start us, length us, event | category | flops | bytes accessed | tf_op | source)
XLA Modules:
  0.0 67.1 jit_solution(7574989448335782895)
XLA Ops:
  1.3 62.9 %radiosity.1 = (f32[16,8,128]{2,1,0:T(8,128)}, f32[16,8,128]{2,1,0:T(8,128)}) custom-call(s32[256]{0:T(256)} %len_h.1, s32[1]{0:T(128)S(6)} %copy.11.count_h, s32[1,256]{1,0:T(1,128)} %bitcast.2, s32[1,256]{1,0:T(1,128)} %bitcast.3, f32[16,8,128]{2,1,0:T(8,128)} %em_h.1, f32[16,8,128]{2,1,0:T(8,128)} %refl_h.1, f32[256,128,128]{2,1,0:T(8,128)} %ff.1), custom_call_target="tpu_custom_call" | custom-call | tf_op jit(solution)/shard_map/radiosity/pallas_call | solution.py:306
  64.2 1.5 %copy.12 = f32[16,8,128]{2,1,0:T(8,128)} copy(f32[16,8,128]{2,1,0:T(8,128)} %get-tuple-element.4) | data formatting | bytes 131072
  65.6 1.5 %copy.13 = f32[16,8,128]{2,1,0:T(8,128)} copy(f32[16,8,128]{2,1,0:T(8,128)} %get-tuple-element.5) | data formatting | bytes 131072

commit v2 on v1

--- a/solution.py
+++ b/solution.py
@@ -9,8 +9,9 @@
 PHASES = 2 * ITERS + 1
 CHUNK = 16
 SLOTS = 4
-UNROLL = 128
-EARLY = 6
+UNROLL = 256
+BEFORE = 2
+EARLY = 9
 
 
 def divide(x, by):
@@ -33,9 +34,9 @@
     return out
 
 
-def kernel(len_h, count_h, source_h, target_h, em_h, refl_h, ff, sol, res,
-           w, stage, runs, vt, outb, inb, dout, din, em, refl, image, direction, total, rs, ds,
-           wout, win, want_s, ints_v, ints_s, reals_v, reals_s, source_v, target_v, len_s, count_s,
+def kernel(count_s, len_h, source_h, target_h, em_h, refl_h, ff, total, res, sol, last_omega,
+           w, stage, runs, vt, outb, inb, dout, din, em, refl, image, direction, rs, ds,
+           wout, win, want_s, ints_v, ints_s, reals_v, reals_s, source_v, target_v, len_v, limit_v, limit_s,
            stage_sem, send_sem, recv_sem, ssend_sem, srecv_sem, wsend_sem, wrecv_sem, small_sem):
     nx, ny = lax.axis_size("gx"), lax.axis_size("gy")
     n = nx * ny
@@ -63,33 +64,30 @@
         return pltpu.make_async_copy(ff.at[pl.ds(c * CHUNK, CHUNK)], stage.at[slot], stage_sem.at[slot])
 
     inputs = [pltpu.make_async_copy(src, dst, small_sem.at[3 + i]) for i, (src, dst) in enumerate((
-        (source_h, source_v), (target_h, target_v), (count_h, count_s), (len_h, len_s), (em_h, em), (refl_h, refl)))]
-    for copy in inputs[:4]:
+        (source_h, source_v), (target_h, target_v), (len_h, len_v), (em_h, em), (refl_h, refl)))]
+    for copy in inputs[:3]:
         copy.start()
     for c in range(min(SLOTS, chunks)):
         fetch(c, c).start()
-    for copy in inputs[4:]:
+    for copy in inputs[3:]:
         copy.start()
 
     lane = lax.broadcasted_iota(i32, (1, 128), 1)
 
-    for copy in inputs[:4]:
+    for copy in inputs[:3]:
         copy.wait()
     owner, slot = divide(source_v[...], clusters)
     target = target_v[...] - me * clusters
     ids = lax.broadcasted_iota(i32, (1, blocks), 1)
     peers = lax.broadcasted_iota(i32, (n, blocks), 0)
-    alive = jnp.broadcast_to(ids < count_s[0], (n, blocks))
+    live = ids < count_s[0]
+    limit_v[...] = jnp.where(live, len_v[...], 0)
+    limits = pltpu.make_async_copy(limit_v, limit_s, small_sem.at[9])
+    limits.start()
+    alive = jnp.broadcast_to(live, (n, blocks))
     match = jnp.logical_and(owner == peers, alive)
     wanted = jnp.max(jnp.where(match, jnp.broadcast_to(slot, (n, blocks)), 0), axis=1, keepdims=True)
     wout[...] = jnp.broadcast_to(wanted, (n, 128)).reshape(n, 1, 128)
-    pl.semaphore_wait(barrier, n - 1)
-
-    each_peer(lambda px, py: pltpu.make_async_remote_copy(
-        src_ref=wout.at[px * ny + py], dst_ref=win.at[me], send_sem=wsend_sem, recv_sem=wrecv_sem,
-        device_id=(px, py), device_id_type=pl.DeviceIdType.MESH).start())
-    win[me] = wout[me]
-
     square_of = (blocks, blocks)
     down = lax.broadcasted_iota(i32, square_of, 0)
     across = lax.broadcasted_iota(i32, square_of, 1)
@@ -122,6 +120,41 @@
     for copy in small:
         copy.start()
 
+    def prepare(c, carry):
+        slot = lax.rem(c, SLOTS)
+        fetch(c, slot).wait()
+
+        def block(b, inner):
+            k = c * CHUNK + b
+            t = stage[slot, b].T
+            limit = limit_s[0, k]
+            j = lax.broadcasted_iota(jnp.int32, (16, cl), 0)
+            error = jnp.zeros((16, cl), f32)
+            for m in range(0, cl, 16):
+                x = jnp.where(j < limit - m, t[m:m + 16] + error, 0.0)
+                q = x.astype(bf16)
+                w[k, m:m + 16] = q
+                error = x - q.astype(f32)
+            return inner
+
+        lax.fori_loop(0, CHUNK, block, 0, unroll=4)
+
+        @pl.when(c + SLOTS < chunks)
+        def _():
+            fetch(c + SLOTS, slot).start()
+
+        return carry
+
+    limits.wait()
+    before = min(BEFORE, chunks)
+    lax.fori_loop(0, before, prepare, 0)
+    pl.semaphore_wait(barrier, n - 1)
+
+    each_peer(lambda px, py: pltpu.make_async_remote_copy(
+        src_ref=wout.at[px * ny + py], dst_ref=win.at[me], send_sem=wsend_sem, recv_sem=wrecv_sem,
+        device_id=(px, py), device_id_type=pl.DeviceIdType.MESH).start())
+    win[me] = wout[me]
+
     def fold(pairs):
         parts = [jnp.sum(a * b, axis=0) for a, b in pairs]
         if len(parts) == 1:
@@ -165,24 +198,27 @@
     def sums(phase, count):
         drain(din.at[phase], srecv_sem.at[phase])
         drain(din.at[phase], ssend_sem.at[phase])
-        column = jnp.sum(din[phase], axis=0)
+        parts = din[phase]
+        column = jnp.sum(parts, axis=0)
         out = []
         for i in range(count):
             part = column if count == 1 else jnp.where(lane // 32 == i, column, 0.0)
             out.append(jnp.broadcast_to(jnp.sum(part, axis=1, keepdims=True), (8, 128)))
-        return out
-
-    def put_sources(v):
+        return out if count == 1 else out + [parts.reshape(n, 128)]
+
+    def put_sources(place, v):
         low = v - v.astype(bf16).astype(f32)
-        vt[...] = jnp.concatenate([v, low], axis=1).astype(bf16)
-
-    def apply(v):
-        blank = jnp.zeros((16, cl), bf16)
-
-        def step(s, acc):
+        vt[place] = jnp.concatenate([v, low], axis=1).astype(bf16)
+
+    def gather(places):
+        tall = 16 * len(places)
+        blank = jnp.zeros((tall, cl), bf16)
+
+        def step(s, accs):
             for u in range(UNROLL // 4):
                 r = s * UNROLL + 4 * u
-                va, vb, vc, vd = (vt[ints_s[1, r + j]] for j in range(4))
+                owners = [ints_s[1, r + j] for j in range(4)]
+                va, vb, vc, vd = (jnp.concatenate([vt[p, o] for p in places], axis=0) for o in owners)
                 wa, wb, wc, wd = (w[ints_s[0, r + j]] for j in range(4))
                 left = jnp.concatenate([
                     jnp.concatenate([va, blank], axis=1), jnp.concatenate([blank, vb], axis=1),
@@ -192,43 +228,22 @@
                 out = jnp.dot(left, right, preferred_element_type=f32)
                 for j in range(4):
                     half = out[:, 0:cl] if j < 2 else out[:, cl:2 * cl]
-                    acc = acc * reals_s[0, r + j] + (half[16 * j:16 * j + 8] + half[16 * j + 8:16 * j + 16])
-                    runs[r + j] = acc
-            return acc
-
-        lax.fori_loop(0, blocks // UNROLL, step, jnp.zeros((8, cl), f32))
-        g = jnp.stack([runs[ints_s[2, t]] * reals_s[1, t] for t in range(clusters)])
-        return v - refl[...] * g
-
-    def prepare(c, carry):
-        slot = lax.rem(c, SLOTS)
-        fetch(c, slot).wait()
-
-        def block(b, inner):
-            k = c * CHUNK + b
-            t = stage[slot, b].T
-            limit = jnp.where(k < count_s[0], len_s[k], 0)
-            j = lax.broadcasted_iota(jnp.int32, (16, cl), 0)
-            error = jnp.zeros((16, cl), f32)
-            for m in range(0, cl, 16):
-                x = jnp.where(j < limit - m, t[m:m + 16] + error, 0.0)
-                q = x.astype(bf16)
-                w[k, m:m + 16] = q
-                error = x - q.astype(f32)
-            return inner
-
-        lax.fori_loop(0, CHUNK, block, 0, unroll=4)
-
-        @pl.when(c + SLOTS < chunks)
-        def _():
-            fetch(c + SLOTS, slot).start()
-
-        return carry
-
-    for copy in inputs[4:]:
+                    new = []
+                    for p, acc in zip(places, accs):
+                        at = tall * j + 16 * len(new)
+                        acc = acc * reals_s[0, r + j] + (half[at:at + 8] + half[at + 8:at + 16])
+                        runs[p, r + j] = acc
+                        new.append(acc)
+                    accs = tuple(new)
+            return accs
+
+        lax.fori_loop(0, blocks // UNROLL, step, tuple(jnp.zeros((8, cl), f32) for _ in places))
+        return [jnp.stack([runs[p, ints_s[2, t]] * reals_s[1, t] for t in range(clusters)]) for p in places]
+
+    for copy in inputs[3:]:
         copy.wait()
     early = min(EARLY, chunks)
-    lax.fori_loop(0, early, prepare, 0)
+    lax.fori_loop(before, early, prepare, 0)
     drain(win, wrecv_sem)
     drain(wout, wsend_sem)
     asked = pltpu.make_async_copy(win, want_s, small_sem.at[2])
@@ -261,37 +276,43 @@
             beta = rho / rho_old * (alpha / omega)
             direction[...] = res[...] + beta * (direction[...] - omega * image[...])
             ds[...] = rs[...] + beta * (ds[...] - omega * inb[2 * it - 1])
-        put_sources(ds[...])
-        image[...] = apply(direction[...])
+        put_sources(0, ds[...])
+        image[...] = direction[...] - refl[...] * gather([0])[0]
         phase = 1 + 2 * it
         send(phase, lambda peer: image[want_s[peer, 0, 0]])
         send_sums(phase, [(em[...], image[...])])
+        put_sources(0, rs[...])
+        receive(phase)
+        put_sources(1, inb[phase])
+        g, h = gather([0, 1])
         if it == 0:
             rho, = sums(0, 1)
-        receive(phase)
         alpha = rho / sums(phase, 1)[0]
-        rs[...] = rs[...] - alpha * inb[phase]
-        put_sources(rs[...])
         res[...] = res[...] - alpha * image[...]
-        sol[...] = apply(res[...])
+        sol[...] = res[...] - refl[...] * (g - alpha * h)
         phase = phase + 1
         if not last:
             send(phase, lambda peer: sol[want_s[peer, 0, 0]])
         send_sums(phase, [(sol[...], res[...]), (sol[...], sol[...]), (em[...], res[...]), (em[...], sol[...])])
+        rs[...] = rs[...] - alpha * inb[phase - 1]
         if it == 0:
             total[...] = alpha * direction[...]
         else:
             total[...] = total[...] + alpha * direction[...]
         if not last:
             receive(phase)
-        tm, tt, sm, st = sums(phase, 4)
+        tm, tt, parts = sums(phase, 2)
         omega = tm / tt
-        rho_old, rho = rho, sm - omega * st
-        total[...] = total[...] + omega * res[...]
-        res[...] = res[...] - omega * sol[...]
         if not last:
+            parts = jnp.sum(parts - omega[0:1] * pltpu.roll(parts, 96, 1), axis=0, keepdims=True)
+            parts = jnp.sum(jnp.where(lane // 32 == 2, parts, 0.0), axis=1, keepdims=True)
+            rho_old, rho = rho, jnp.broadcast_to(parts, (8, 128))
+        if last:
+            last_omega[...] = omega
+        else:
+            total[...] = total[...] + omega * res[...]
+            res[...] = res[...] - omega * sol[...]
             rs[...] = rs[...] - omega * inb[phase]
-    sol[...] = total[...]
 
 
 def local(emission, reflectance, form_factors, link_source, link_target, link_length, block_count):
@@ -303,21 +324,20 @@
     field = (clusters, bands, cl)
     rows = (devices, bands, cl)
     dma = pltpu.SemaphoreType.DMA
-    return pl.pallas_call(
+    total, middle, bounce, omega = pl.pallas_call(
         kernel,
-        out_shape=[jax.ShapeDtypeStruct(field, f32)] * 2,
-        in_specs=[pl.BlockSpec(memory_space=pl.ANY)] * 7,
-        out_specs=[vmem, vmem],
+        out_shape=[jax.ShapeDtypeStruct(field, f32)] * 3 + [jax.ShapeDtypeStruct((bands, cl), f32)],
+        in_specs=[pl.BlockSpec(memory_space=pltpu.SMEM)] + [pl.BlockSpec(memory_space=pl.ANY)] * 6,
+        out_specs=[vmem] * 4,
         scratch_shapes=[
             pltpu.VMEM((blocks, cl, cl), bf16),
             pltpu.VMEM((SLOTS, CHUNK, cl, cl), f32),
-            pltpu.VMEM((blocks, bands, cl), f32),
-            pltpu.VMEM((devices, 2 * bands, cl), bf16),
+            pltpu.VMEM((2, blocks, bands, cl), f32),
+            pltpu.VMEM((2, devices, 2 * bands, cl), bf16),
             pltpu.VMEM((PHASES - 1, devices, bands, cl), f32),
             pltpu.VMEM((PHASES - 1, devices, bands, cl), f32),
             pltpu.VMEM((PHASES, 1, 128), f32),
             pltpu.VMEM((PHASES, devices, 1, 128), f32),
-            pltpu.VMEM(field, f32),
             pltpu.VMEM(field, f32),
             pltpu.VMEM(field, f32),
             pltpu.VMEM(field, f32),
@@ -333,8 +353,9 @@
             pltpu.SMEM((8, blocks), f32),
             pltpu.VMEM((1, blocks), i32),
             pltpu.VMEM((1, blocks), i32),
-            pltpu.SMEM((blocks,), i32),
-            pltpu.SMEM((1,), i32),
+            pltpu.VMEM((1, blocks), i32),
+            pltpu.VMEM((1, blocks), i32),
+            pltpu.SMEM((1, blocks), i32),
             dma((SLOTS,)),
             dma((PHASES - 1,)),
             dma((PHASES - 1,)),
@@ -342,16 +363,18 @@
             dma((PHASES,)),
             dma,
             dma,
-            dma((9,)),
+            dma((10,)),
         ],
         compiler_params=pltpu.CompilerParams(
             collective_id=0, has_side_effects=True, vmem_limit_bytes=VMEM_LIMIT),
         name="radiosity",
-    )(link_length, block_count, link_source.reshape(1, blocks), link_target.reshape(1, blocks),
-      emission, reflectance, form_factors)
-
-
-VMEM_LIMIT = 56 * 1024 * 1024
+    )(block_count, *(pltpu.with_memory_space_constraint(x, pltpu.HBM) for x in (
+        link_length.reshape(1, blocks), link_source.reshape(1, blocks), link_target.reshape(1, blocks),
+        emission, reflectance, form_factors)))
+    return total + omega * middle, middle - omega * bounce
+
+
+VMEM_LIMIT = 24 * 1024 * 1024
 
 
 def solution(mesh):

time: 67.3 us -> 60.6 us (0.900)
  Pallas kernels: 62.9 us -> 58.5 us
  local copies, waits for them, and re-layouts: 2.95 us -> 0 us
    pallas_call x1, Pallas kernels: 62.9 us -> 58.5 us  [local(): pl.pallas_call(kernel, out_shape=[jax.ShapeDtypeStruct(field, f32)] * 3 +...]
    unnamed x2 -> x0, local copies, waits for them, and re-layouts: 2.95 us -> none
where the time goes in v2:
time: 60.6 us; the launch traced here: 60.4 us
  Pallas kernels  58.5 us (97%)
  between operations  1.29 us (2%)
  other arithmetic  0.67 us (1%)
    pallas_call x1, Pallas kernels, local(): pl.pallas_call(kernel, out_shape=[jax.ShapeDtypeStruct(field, f32)] * 3 +...  58.5 us

profile of v2, /device:TPU:0, one launch (start us, length us, event | category | flops | bytes accessed | tf_op | source)
XLA Modules:
  0.0 60.4 jit_solution(2927373155760243849)
XLA Ops:
  1.3 58.5 %radiosity.1 = (f32[16,8,128]{2,1,0:T(8,128)S(1)}, f32[16,8,128]{2,1,0:T(8,128)S(1)}, f32[16,8,128]{2,1,0:T(8,128)S(1)}, f32[8,128]{1,0:T(8,128)S(1)}) custom-call(s32[1]{0:T(128)S(6)} %copy.9.count_s, s32[1,256]{1,0:T(1,128)} %bitcast.3, s32[1,256]{1,0:T(1,128)} %bitcast.4, s32[1,256]{1,0:T(1,128)} %bitcast.5, f32[16,8,128]{2,1,0:T(8,128)} %em_h.1, ...), custom_call_target="tpu_custom_call" | custom-call | tf_op jit(solution)/shard_map/radiosity/pallas_call | solution.py:327
  59.7 0.7 %multiply_subtract_fusion = (f32[16,8,128]{2,1,0:T(8,128)}, f32[16,8,128]{2,1,0:T(8,128)}) fusion(f32[16,8,128]{2,1,0:T(8,128)S(1)} %get-tuple-element.8, f32[16,8,128]{2,1,0:T(8,128)S(1)} %get-tuple-element.9, f32[8,128]{1,0:T(8,128)S(1)} %get-tuple-element.7, f32[16,8,128]{2,1,0:T(8,128)S(1)} %get-tuple-element.6), kind=kLoop, calls=%fused_computation | loop fusion | flops 65536 | bytes 331776 | tf_op jit(solution)/shard_map/sub | solution.py:374
